TPU v7x, 128 devices: a whole 4x4x4 slice. The times are simulated.
128 devices in a mesh: ka: 32 (over z, y, core), col: 4 (over x).
Axes of the slice: x: 4, y: 4, z: 4, core: 2. Of those that a mesh axis runs over, the one named last changes fastest.
Arguments:
- hamiltonian: bfloat16 [1024, 2, 9216], P(('ka', 'col')), may hold values from -0.1875 to 0.1875
- eigvecs: bfloat16 [2048, 2, 96, 96], P('ka'), may hold values from -0.625 to 0.625
- spin: bfloat16 [2, 96, 96], replicated, may hold values from -0.059814453 to 0.059814453
- k_indices: int32 [2048, 3], P('ka'), may hold values from 0 to 63
- r_vectors: int32 [1024, 3], replicated, may hold values from -5 to 5, as said below
- degeneracy: int32 [1024], replicated, may hold values from 1 to 4
- fermi_level: float32 [1], replicated, may hold values from -0.5 to 0.5
Outputs:
- band_curvature: float32 [9, 96, 2048], P(None, None, ('ka', 'col'))
- conductivity: float32 [9, 96], replicated
Inputs may be any that keep to these rules, and one draw needn't show every extreme that they name: `r_vectors`: the 1024 lattice vectors are all distinct.
All inputs are finite; a program needn't handle non-finite values.
Results may differ from a plain program's by a relative error of at most 0.0085.
The roundings to bfloat16 on the way count: a program that leaves them out, or rounds other values in their place, can miss the bound.
Values may be sent and summed in bfloat16 or wider, within the bound.
No kernel may reach another device: no remote copies, remote signals or barrier semaphores. Data moves between devices by JAX's collectives and lax.ppermute only.
A program may use at most 128 MiB of HBM per device.

v0:
```python
import math
import jax
import jax.numpy as jnp
from jax import lax
from jax.sharding import PartitionSpec as P

WF = 96
GRID = 64
two_pi = 2.0 * math.pi
broadening = 0.5
smearing = 0.1


def sent_to_all(value, axis):
    copies = jnp.broadcast_to(value, (lax.axis_size(axis), *value.shape))
    return lax.all_to_all(copies, axis, split_axis=0, concat_axis=0, tiled=True)


def taken_together(value, axis):
    everything = sent_to_all(value, axis)
    return jnp.sum(everything, axis=0)


def phase_rows(kpoints, lattice, degrees, height):
    flat_index = jnp.arange(height, dtype=jnp.int32)
    vector_index = flat_index // 2
    halves = flat_index % 2
    lattice_rows = jnp.take(lattice, vector_index, axis=0)
    degree_rows = jnp.take(degrees, vector_index, axis=0)
    lattice_dot = jnp.mod(jnp.sum(kpoints[:, None, :] * lattice_rows[None, :, :], axis=-1), GRID)
    angles = lattice_dot.astype(jnp.float32) * (two_pi / GRID)
    cosine = jnp.cos(angles)
    sine_part = jnp.sin(angles)
    inverse = 1.0 / degree_rows.astype(jnp.float32)
    coords = lattice_rows.astype(jnp.float32) * inverse[:, None]
    real_part = jnp.stack(
        [
            cosine * inverse,
            -sine_part * coords[:, 0],
            -sine_part * coords[:, 1],
            -sine_part * coords[:, 2],
        ],
        axis=1,
    )
    imag_part = jnp.stack(
        [sine_part * inverse, cosine * coords[:, 0], cosine * coords[:, 1], cosine * coords[:, 2]],
        axis=1,
    )
    real_rows = (halves == 0)[None, None, :]
    top_rows = jnp.where(real_rows, real_part, -imag_part)
    low_rows = jnp.where(real_rows, imag_part, real_part)
    return jnp.stack([top_rows, low_rows], axis=2)


def rotate(operators, vectors):
    ops_re = operators[:, :, 0]
    ops_im = operators[:, :, 1]
    vec_re = vectors[:, 0]
    vec_im = vectors[:, 1]
    half_re = jnp.einsum(
        "kcij,kjm->kcim", ops_re, vec_re, preferred_element_type=jnp.float32
    ) - jnp.einsum("kcij,kjm->kcim", ops_im, vec_im, preferred_element_type=jnp.float32)
    half_im = jnp.einsum(
        "kcij,kjm->kcim", ops_re, vec_im, preferred_element_type=jnp.float32
    ) + jnp.einsum("kcij,kjm->kcim", ops_im, vec_re, preferred_element_type=jnp.float32)
    half_re = half_re.astype(jnp.bfloat16)
    half_im = half_im.astype(jnp.bfloat16)
    full_re = jnp.einsum(
        "kjn,kcjm->kcnm", vec_re, half_re, preferred_element_type=jnp.float32
    ) + jnp.einsum("kjn,kcjm->kcnm", vec_im, half_im, preferred_element_type=jnp.float32)
    full_im = jnp.einsum(
        "kjn,kcjm->kcnm", vec_re, half_im, preferred_element_type=jnp.float32
    ) - jnp.einsum("kjn,kcjm->kcnm", vec_im, half_re, preferred_element_type=jnp.float32)
    sym_re = (full_re + jnp.swapaxes(full_re, -1, -2)) * 0.5
    sym_im = (full_im - jnp.swapaxes(full_im, -1, -2)) * 0.5
    return jnp.stack([sym_re, sym_im], axis=2).astype(jnp.bfloat16)


def kubo(bloch_ops, spin_bloch, fermi_level):
    energy = jnp.diagonal(bloch_ops[:, 0, 0].astype(jnp.float32), axis1=-2, axis2=-1)
    velo_re = bloch_ops[:, 1:, 0].astype(jnp.float32)
    velo_im = bloch_ops[:, 1:, 1].astype(jnp.float32)
    spin_re = spin_bloch[:, 0].astype(jnp.float32)
    spin_im = spin_bloch[:, 1].astype(jnp.float32)
    prod_re = jnp.einsum("kij,kajm->kaim", spin_re, velo_re) - jnp.einsum(
        "kij,kajm->kaim", spin_im, velo_im
    )
    prod_im = jnp.einsum("kij,kajm->kaim", spin_re, velo_im) + jnp.einsum(
        "kij,kajm->kaim", spin_im, velo_re
    )
    cur_re = (prod_re + jnp.swapaxes(prod_re, -1, -2)) * 0.5
    cur_im = (prod_im - jnp.swapaxes(prod_im, -1, -2)) * 0.5
    energy_gap = energy[:, :, None] - energy[:, None, :]
    weight = 1.0 / (energy_gap * energy_gap + broadening * broadening)
    curvature = -2.0 * (
        jnp.einsum("kanm,kbmn,knm->kabn", cur_re, velo_im, weight)
        + jnp.einsum("kanm,kbmn,knm->kabn", cur_im, velo_re, weight)
    )
    occupation = 1.0 / (1.0 + jnp.exp((energy - fermi_level[0]) / smearing))
    weighted = jnp.einsum("kn,kabn->abn", occupation, curvature)
    return (curvature, weighted)


def on_device(hamiltonian, eigvecs, spin, k_indices, r_vectors, degeneracy, fermi_level):
    kcount = eigvecs.shape[0]
    col_count = lax.axis_size("col")
    quarter = kcount // col_count
    column = lax.axis_index("col")
    vectors = lax.dynamic_slice_in_dim(eigvecs, column * quarter, quarter, 0)
    flat_shard = hamiltonian.reshape(hamiltonian.shape[0] * 2, WF * WF)
    entry_width = WF * WF // col_count
    entry_slice = lax.all_to_all(flat_shard, "col", split_axis=1, concat_axis=0, tiled=True)
    segment = lax.all_gather(entry_slice, "ka", axis=0, tiled=True)
    height = segment.shape[0]
    phases = phase_rows(k_indices, r_vectors, degeneracy, height)
    phases = phases.reshape(kcount * 8, height).astype(jnp.bfloat16)
    summed = jnp.dot(phases, segment, preferred_element_type=jnp.float32)
    summed = summed.reshape(kcount, 4, 2, entry_width)
    own_entries = summed.astype(jnp.bfloat16)
    regrouped = lax.all_to_all(own_entries, "col", split_axis=0, concat_axis=3, tiled=True)
    interpolated = regrouped.reshape(quarter, 4, 2, WF, WF)
    bloch_ops = rotate(interpolated, vectors)
    spin_wide = spin.astype(jnp.float32)
    spin_sym = jnp.stack(
        [(spin_wide[0] + spin_wide[0].T) * 0.5, (spin_wide[1] - spin_wide[1].T) * 0.5]
    ).astype(jnp.bfloat16)
    spin_ops = jnp.broadcast_to(spin_sym[None, None], (quarter, 1, 2, WF, WF))
    spin_bloch = rotate(spin_ops, vectors)[:, 0]
    curvature, weighted = kubo(bloch_ops, spin_bloch, fermi_level)
    total_points = kcount * lax.axis_size("ka")
    partial_value = weighted.reshape(9, WF) / math.sqrt(total_points)
    totals = taken_together(taken_together(partial_value, "col"), "ka")
    band_out = jnp.transpose(curvature, (1, 2, 3, 0)).reshape(9, WF, quarter)
    return (band_out, totals)


def solution(mesh):
    in_specs = (
        P(("ka", "col"), None, None),
        P("ka", None, None, None),
        P(),
        P("ka", None),
        P(),
        P(),
        P(),
    )
    out_specs = (P(None, None, ("ka", "col")), P())
    return jax.shard_map(
        on_device, mesh=mesh, in_specs=in_specs, out_specs=out_specs, check_vma=False
    )
```

profile of v0, /device:TPU:1, one launch (start us, length us, event | category | flops | bytes accessed | tf_op | source)
XLA Modules:
  0.0 234.4 jit_solution(3155142561728896138)
XLA Ops:
  7.2 1.3 all_to_all.31
  8.6 10.6 %all_to_all.44 = bf16[16,4,2304]{2,0,1:T(8,128)(2,1)} all-to-all(bf16[16,4,2304]{2,0,1:T(8,128)(2,1)S(1)} %copy.186), channel_id=1, replica_groups=mesh['ka'=32,'col'=4] {'col'}, dimensions={1} | all-to-all | bytes 589824 | tf_op jit(solution)/shard_map/all_to_all | solution.py:112
  19.2 0.8 convert_element_type.177
  20.0 0.7 slice.86
  20.8 1.7 copy.184
  22.6 8.6 %gather_fusion.1 = s32[2048]{0:T(1024)S(1)} fusion(s32[1024]{0:T(1024)S(1)} %copy-done.2, s32[2048]{0:T(1024)S(1)} %broadcast_clamp_fusion), kind=kCustom, calls=%fused_computation.1 | custom fusion | bytes 24576 | tf_op jit(solution)/shard_map/jit(_take)/gather | solution.py:29
  31.1 8.6 %gather_fusion = s32[2048,3]{1,0:T(8,128)} fusion(s32[1024,3]{1,0:T(8,128)} %copy.184, s32[2048]{0:T(1024)S(1)} %broadcast_clamp_fusion), kind=kCustom, calls=%fused_computation | custom fusion | bytes 57344 | tf_op jit(solution)/shard_map/jit(_take)/gather | solution.py:28
  39.8 2.7 %convert_multiply_fusion = (f32[2048,3]{1,0:T(8,128)}, s32[2048,3]{1,0:T(8,128)}) fusion(f32[2048]{0:T(1024)S(1)} %convert_divide_fusion, s32[2048,3]{1,0:T(8,128)} %gather_fusion, pred[2048]{0:T(1024)(128)(4,1)S(1)} %fusion.93), kind=kLoop, calls=%fused_computation.55 | loop fusion | flops 18432 | bytes 83968 | tf_op jit(solution)/shard_map/mul | solution.py:35
  42.5 1.6 copy.185
  44.5 3.5 %slice_reduce_fusion.2 = (f32[2048]{0:T(1024)S(1)}, f32[2048]{0:T(1024)S(1)}, f32[2048]{0:T(1024)S(1)}) fusion(f32[2048,3]{1,0:T(8,128)} %get-tuple-element.5), kind=kLoop, calls=%fused_computation.54 | loop fusion | bytes 49152 | tf_op jit(solution)/shard_map/slice | solution.py:39
  48.9 1.2 fusion.42
  50.1 2.2 multiply_bitcast_fusion.7
  52.4 2.2 multiply_bitcast_fusion.3
  54.5 1.6 select_convert_fusion.1
  56.1 20.9 %all-gather.2.cloned.1.call-done = bf16[2048,2304]{1,0:T(8,128)(2,1)} async-done(((bf16[64,2304]{1,0:T(8,128)(2,1)}), bf16[2048,2304]{1,0:T(8,128)(2,1)}) %all-gather.2.cloned.1.call-update) | async-done | bytes 9437200 | tf_op jit(solution)/shard_map/all_gather | solution.py:113
  77.1 9.3 %fusion.2 = bf16[64,4,2,2304]{3,0,2,1:T(8,128)(2,1)S(1)} fusion(bf16[2048,2304]{1,0:T(8,128)(2,1)} %all-gather.2.cloned.1.call-done, bf16[64,4,1,2048]{3,0,2,1:T(8,128)(2,1)} %get-tuple-element.8, bf16[64,4,1,2048]{3,0,2,1:T(8,128)(2,1)} %get-tuple-element.7), kind=kOutput, calls=%fused_computation.5 | convolution fusion | flops 4834066432 | bytes 13893632 | tf_op jit(solution)/shard_map/dot_general | solution.py:117
  86.4 3.8 %copy.187 = bf16[64,4,2,2304]{3,2,1,0:T(2,128)(2,1)} copy(bf16[64,4,2,2304]{3,0,2,1:T(8,128)(2,1)S(1)} %fusion.2) | data formatting | bytes 4718592 | tf_op jit(solution)/shard_map/convert_element_type | solution.py:119
  90.2 4.7 %all-to-all-start.1 = ((bf16[64,4,2,2304]{3,2,1,0:T(2,128)(2,1)}), bf16[64,4,2,2304]{3,2,1,0:T(2,128)(2,1)}, u32[]{:S(2)}, u32[]{:S(2)}) async-start(bf16[64,4,2,2304]{3,2,1,0:T(2,128)(2,1)} %copy.187), calls=%async_computation.1 | async-start | bytes 4718592 | tf_op jit(solution)/shard_map/all_to_all | solution.py:120
  94.9 1.1 fusion.37
  96.0 1.0 fusion.24
  97.0 0.8 copy-done.14
  97.7 1.2 fusion.22
  99.0 2.3 copy.203
  101.3 1.3 fusion.45
  102.6 1.2 convolution_subtract_fusion.2
  103.8 2.3 copy.207
  106.9 2.2 fusion.34
  109.2 14.5 %all-to-all-done.1 = bf16[64,4,2,2304]{3,2,1,0:T(2,128)(2,1)} async-done(((bf16[64,4,2,2304]{3,2,1,0:T(2,128)(2,1)}), bf16[64,4,2,2304]{3,2,1,0:T(2,128)(2,1)}, u32[]{:S(2)}, u32[]{:S(2)}) %all-to-all-start.1) | async-done | bytes 2359328 | tf_op jit(solution)/shard_map/all_to_all | solution.py:120
  123.7 5.0 %copy.260 = bf16[4,16,4,2,2304]{4,0,2,1,3:T(4,128)(2,1)} copy(bf16[4,16,4,2,2304]{4,3,2,1,0:T(2,128)(2,1)} %bitcast.16) | data formatting | bytes 4718592 | tf_op jit(solution)/shard_map/all_to_all | solution.py:120
  128.7 7.4 %reshape.803 = bf16[16,4,2,96,96]{4,3,1,0,2:T(8,128)(2,1)} reshape(bf16[16,4,2,4,2304]{4,3,1,0,2:T(4,128)(2,1)} %bitcast.234) | data formatting | bytes 4718592 | tf_op jit(solution)/shard_map/reshape | solution.py:121
  136.1 2.1 fusion.21
  138.5 0.6 fusion.20
  139.0 0.6 add_convert_fusion
  139.6 0.6 fusion.52
  140.8 0.6 subtract_convert_fusion
  141.4 2.3 fusion.49
  143.6 2.3 convolution_subtract_fusion
  145.9 3.6 %copy.192 = f32[16,4,96,96]{2,3,1,0:T(8,128)} copy(f32[16,4,96,96]{3,2,1,0:T(8,128)} %convolution_subtract_fusion) | data formatting | bytes 4718592 | tf_op jit(solution)/shard_map/sub | solution.py:71
  149.5 4.7 %convolution_add_fusion = f32[16,4,96,96]{3,2,1,0:T(8,128)} fusion(f32[16,4,96,96]{3,2,1,0:T(8,128)} %fusion.49, bf16[16,4,96,96]{3,2,1,0:T(8,128)(2,1)} %copy-done.10, bf16[64,2,96,96]{3,2,1,0:T(8,128)(2,1)S(1)} %copy-done, s32[]{:T(128)S(6)} %select_n.239, s32[]{:T(128)S(6)} %add.272), kind=kOutput, calls=%fused_computation.32 | convolution fusion | flops 113836032 | bytes 6291464 | tf_op jit(solution)/shard_map/kjn,kcjm->kcnm/dot_general | solution.py:70
  154.1 3.8 %copy.195 = f32[16,4,96,96]{3,2,1,0:T(8,128)} copy(f32[16,4,96,96]{2,3,1,0:T(8,128)} %bitcast.232) | data formatting | bytes 4718592 | tf_op jit(solution)/shard_map/add | solution.py:68
  157.9 5.3 %fusion.18 = (bf16[16,4,1,96,96]{4,3,1,0,2:T(8,128)(2,1)S(1)}, bf16[16,4,1,96,96]{4,3,1,0,2:T(8,128)(2,1)S(1)}) fusion(f32[16,4,96,96]{3,2,1,0:T(8,128)} %copy.195, f32[16,4,96,96]{3,2,1,0:T(8,128)} %convolution_add_fusion, f32[16,4,96,96]{3,2,1,0:T(8,128)S(1)} %copy-done.3, f32[16,4,96,96]{2,3,1,0:T(8,128)} %copy.192), kind=kLoop, calls=%fused_computation.36 | loop fusion | flops 3538944 | bytes 11796480 | tf_op jit(solution)/shard_map/stack | solution.py:76
  163.3 1.1 fusion.36
  164.9 1.9 fusion.25
  166.8 0.5 convolution_subtract_fusion.1
  167.3 2.0 copy.209
  169.3 3.3 %fusion.12 = bf16[16,3,96,96]{3,2,1,0:T(8,128)(2,1)} fusion(f32[16,3,96,96]{3,2,1,0:T(8,128)S(1)} %convolution_subtract_fusion.1, f32[16,3,96,96]{2,3,1,0:T(8,128)} %copy.209), kind=kLoop, calls=%fused_computation.21 | loop fusion | flops 1327104 | bytes 4423680 | tf_op jit(solution)/shard_map/mul | solution.py:91
  172.7 0.5 convolution_add_fusion.1
  173.2 2.0 copy.214
  175.2 3.1 %subtract_multiply_fusion = bf16[16,3,96,96]{3,2,1,0:T(8,128)(2,1)} fusion(f32[16,3,96,96]{3,2,1,0:T(8,128)} %copy.214, f32[16,3,96,96]{3,2,1,0:T(8,128)S(1)} %convolution_add_fusion.1), kind=kLoop, calls=%fused_computation.24 | loop fusion | flops 1327104 | bytes 4423680 | tf_op jit(solution)/shard_map/mul | solution.py:92
  178.3 4.0 %copy.196 = f32[16,96,96]{0,2,1:T(8,128)} copy(f32[16,96,96]{2,1,0:T(8,128)} %fusion.36) | data formatting | bytes 1179648 | tf_op jit(solution)/shard_map/convert_element_type | solution.py:80
  182.2 3.0 %gather_fusion.2 = f32[96,16]{1,0:T(8,128)S(1)} fusion(f32[16,96,96]{0,2,1:T(8,128)} %copy.196, s32[96]{0:T(128)S(1)} %or_bitcast_fusion), kind=kCustom, calls=%fused_computation.2 | custom fusion | bytes 13056 | tf_op jit(solution)/shard_map/jit(diagonal)/gather | solution.py:80
  185.6 2.0 bitcast_multiply_fusion.2
  187.5 2.8 %copy.215 = bf16[16,96,96,3]{2,3,1,0:T(4,128)(2,1)S(1)} copy(bf16[16,96,96,3]{1,2,3,0:T(8,128)(2,1)} %get-tuple-element.10) | data formatting | bytes 1769472 | tf_op jit(solution)/shard_map/kanm,kbmn,knm->kabn/dot_general | solution.py:97
  190.4 3.9 %copy.210 = bf16[16,96,96,3]{2,3,1,0:T(4,128)(2,1)} copy(bf16[16,96,96,3]{1,2,3,0:T(8,128)(2,1)} %get-tuple-element.9) | data formatting | bytes 1769472 | tf_op jit(solution)/shard_map/kanm,kbmn,knm->kabn/dot_general | solution.py:96
  194.3 1.8 fusion.8
  196.1 5.7 %fusion.5 = (f32[96,3,3]{1,2,0:T(4,128)S(1)}, f32[16,96,3,3]{3,2,1,0:T(4,128)}) fusion(f32[96,16]{0,1:T(8,128)S(1)} %divide_bitcast_fusion, f32[16,96,3,3]{3,2,1,0:T(4,128)S(1)} %fusion.8, bf16[16,96,96,3]{2,3,1,0:T(4,128)(2,1)S(1)} %copy-done.18, bf16[16,3,96,96]{3,2,1,0:T(8,128)(2,1)S(1)} %copy-done.19), kind=kOutput, calls=%fused_computation.7 | convolution fusion | flops 2708640 | bytes 1889664 | tf_op jit(solution)/shard_map/kanm,kbmn,knm->kabn/dot_general | solution.py:96
  202.0 6.5 %all_to_all.45 = f32[4,1,864]{2,1,0:T(1,128)S(1)} all-to-all(f32[4,1,864]{2,1,0:T(1,128)S(1)} %reshape.838), channel_id=1, replica_groups=mesh['ka'=32,'col'=4] {'col'}, dimensions={0} | all-to-all | bytes 27648 | tf_op jit(solution)/shard_map/all_to_all | solution.py:16
  209.1 0.7 reduce.8
  209.9 0.8 reshape.840
  210.7 7.7 %all-to-all-start.3 = ((f32[32,1,864]{2,1,0:T(1,128)}), f32[32,1,864]{2,1,0:T(1,128)S(1)}, u32[]{:S(2)}, u32[]{:S(2)}) async-start(f32[32,1,864]{2,1,0:T(1,128)} %reshape.840), calls=%async_computation.3 | async-start | bytes 229376 | tf_op jit(solution)/shard_map/all_to_all | solution.py:16
  218.4 2.9 %copy.217 = f32[3,3,96,16]{2,3,1,0:T(8,128)} copy(f32[3,3,96,16]{0,1,2,3:T(4,128)} %bitcast.236) | data formatting | bytes 110592 | tf_op jit(solution)/shard_map/mul | solution.py:95
  221.3 4.6 %all-to-all-done.3 = f32[32,1,864]{2,1,0:T(1,128)S(1)} async-done(((f32[32,1,864]{2,1,0:T(1,128)}), f32[32,1,864]{2,1,0:T(1,128)S(1)}, u32[]{:S(2)}, u32[]{:S(2)}) %all-to-all-start.3) | async-done | bytes 110624 | tf_op jit(solution)/shard_map/all_to_all | solution.py:16
  225.9 0.9 reduce.9
  226.9 0.6 reduce_sum.32
  (76 shorter events, 4.1 us)
Async XLA Ops:
  7.2 40.9 %copy-start = (bf16[64,2,96,96]{3,2,1,0:T(8,128)(2,1)S(1)}, bf16[64,2,96,96]{3,2,1,0:T(8,128)(2,1)}, u32[]{:S(2)}) copy-start(bf16[64,2,96,96]{3,2,1,0:T(8,128)(2,1)} %param.8) | copy-start | bytes 7077892
  7.2 15.4 %copy-start.2 = (s32[1024]{0:T(1024)S(1)}, s32[1024]{0:T(1024)}, u32[]{:S(2)}) copy-start(s32[1024]{0:T(1024)} %param.12) | copy-start | bytes 12292
  7.2 69.9 %all-gather.2.cloned.1.call-start = ((), (), s32[]{:S(2)}) async-start(), calls=%async_computation.4 | async-start | bytes 9732096 | tf_op jit(solution)/shard_map/all_gather | solution.py:113
  39.8 4.5 %copy-start.22 = (s32[64,3]{0,1:T(4,128)S(1)}, s32[64,3]{0,1:T(4,128)}, u32[]{:S(2)}) copy-start(s32[64,3]{0,1:T(4,128)} %param.10) | copy-start | bytes 2308
  48.0 0.6 copy-start.21
  48.0 4.3 %copy-start.20 = (bf16[96,96]{1,0:T(8,128)(2,1)}, bf16[96,96]{1,0:T(8,128)(2,1)S(1)}, u32[]{:S(2)}) copy-start(bf16[96,96]{1,0:T(8,128)(2,1)S(1)} %get-tuple-element.19) | copy-start | bytes 55300
  90.2 33.5 %all-to-all-start.1 = ((bf16[64,4,2,2304]{3,2,1,0:T(2,128)(2,1)}), bf16[64,4,2,2304]{3,2,1,0:T(2,128)(2,1)}, u32[]{:S(2)}, u32[]{:S(2)}) async-start(bf16[64,4,2,2304]{3,2,1,0:T(2,128)(2,1)} %copy.187), calls=%async_computation.1 | async-start | bytes 4718592 | tf_op jit(solution)/shard_map/all_to_all | solution.py:120
  94.9 2.9 %copy-start.16 = (f32[16,96,96]{2,1,0:T(8,128)S(1)}, f32[16,96,96]{2,1,0:T(8,128)}, u32[]{:S(2)}) copy-start(f32[16,96,96]{2,1,0:T(8,128)} %fusion.42) | copy-start | bytes 1769476
  97.0 0.8 copy-start.14
  106.1 3.0 %copy-start.12 = (f32[16,96,96]{2,1,0:T(8,128)S(1)}, f32[16,96,96]{2,1,0:T(8,128)}, u32[]{:S(2)}) copy-start(f32[16,96,96]{2,1,0:T(8,128)} %convolution_subtract_fusion.2) | copy-start | bytes 1769476
  106.1 3.0 %copy-start.17 = (f32[16,1,96,96]{3,2,0,1:T(8,128)S(1)}, f32[16,1,96,96]{3,2,0,1:T(8,128)}, u32[]{:S(2)}) copy-start(f32[16,1,96,96]{3,2,0,1:T(8,128)} %copy.207) | copy-start | bytes 1769476
  136.1 2.4 %copy-start.4 = (bf16[16,4,2,96,96]{4,3,1,0,2:T(8,128)(2,1)S(1)}, bf16[16,4,2,96,96]{4,3,1,0,2:T(8,128)(2,1)}, u32[]{:S(2)}) copy-start(bf16[16,4,2,96,96]{4,3,1,0,2:T(8,128)(2,1)} %reshape.803) | copy-start | bytes 7077892
  139.6 1.1 copy-start.10
  154.1 3.8 %copy-start.3 = (f32[16,4,96,96]{3,2,1,0:T(8,128)S(1)}, f32[16,4,96,96]{3,2,1,0:T(8,128)}, u32[]{:S(2)}) copy-start(f32[16,4,96,96]{3,2,1,0:T(8,128)} %convolution_subtract_fusion) | copy-start | bytes 7077892
  157.9 6.4 %copy-start.15 = (bf16[16,96,96,1]{2,1,3,0:T(8,128)(2,1)S(1)}, bf16[16,96,96,1]{2,1,3,0:T(8,128)(2,1)}, u32[]{:S(2)}) copy-start(bf16[16,96,96,1]{2,1,3,0:T(8,128)(2,1)} %fusion.34) | copy-start | bytes 884740
  163.2 1.6 copy-start.5
  163.2 3.6 %copy-start.8 = (bf16[16,4,1,96,96]{4,3,1,0,2:T(8,128)(2,1)}, bf16[16,4,1,96,96]{4,3,1,0,2:T(8,128)(2,1)S(1)}, u32[]{:S(2)}) copy-start(bf16[16,4,1,96,96]{4,3,1,0,2:T(8,128)(2,1)S(1)} %get-tuple-element.24) | copy-start | bytes 3538948
  169.3 3.4 %copy-start.6 = (bf16[16,4,1,96,96]{4,3,1,0,2:T(8,128)(2,1)S(1)}, bf16[16,4,1,96,96]{4,3,1,0,2:T(8,128)(2,1)}, u32[]{:S(2)}) copy-start(bf16[16,4,1,96,96]{4,3,1,0,2:T(8,128)(2,1)} %copy-done.5) | copy-start | bytes 3538948
  169.3 3.4 %copy-start.11 = (f32[16,3,96,96]{3,2,1,0:T(8,128)S(1)}, f32[16,3,96,96]{3,2,1,0:T(8,128)}, u32[]{:S(2)}) copy-start(f32[16,3,96,96]{3,2,1,0:T(8,128)} %fusion.25) | copy-start | bytes 5308420
  178.3 7.3 %copy-start.7 = (bf16[16,4,1,96,96]{4,3,1,0,2:T(8,128)(2,1)S(1)}, bf16[16,4,1,96,96]{4,3,1,0,2:T(8,128)(2,1)}, u32[]{:S(2)}) copy-start(bf16[16,4,1,96,96]{4,3,1,0,2:T(8,128)(2,1)} %copy-done.5) | copy-start | bytes 3538948
  178.3 7.3 %copy-start.9 = (bf16[16,4,1,96,96]{4,3,1,0,2:T(8,128)(2,1)S(1)}, bf16[16,4,1,96,96]{4,3,1,0,2:T(8,128)(2,1)}, u32[]{:S(2)}) copy-start(bf16[16,4,1,96,96]{4,3,1,0,2:T(8,128)(2,1)} %copy-done.8) | copy-start | bytes 3538948
  187.5 6.7 %copy-start.13 = (bf16[16,3,96,96]{3,2,1,0:T(8,128)(2,1)S(1)}, bf16[16,3,96,96]{3,2,1,0:T(8,128)(2,1)}, u32[]{:S(2)}) copy-start(bf16[16,3,96,96]{3,2,1,0:T(8,128)(2,1)} %subtract_multiply_fusion) | copy-start | bytes 2654212
  194.3 1.8 copy-start.18
  194.3 1.8 copy-start.19
  209.9 17.7 %copy-start.1 = (bf16[64,2,96,96]{3,2,1,0:T(8,128)(2,1)S(1)}, bf16[64,2,96,96]{3,2,1,0:T(8,128)(2,1)}, u32[]{:S(2)}) copy-start(bf16[64,2,96,96]{3,2,1,0:T(8,128)(2,1)} %param.8) | copy-start | bytes 7077892
  210.7 15.1 %all-to-all-start.3 = ((f32[32,1,864]{2,1,0:T(1,128)}), f32[32,1,864]{2,1,0:T(1,128)S(1)}, u32[]{:S(2)}, u32[]{:S(2)}) async-start(f32[32,1,864]{2,1,0:T(1,128)} %reshape.840), calls=%async_computation.3 | async-start | bytes 229376 | tf_op jit(solution)/shard_map/all_to_all | solution.py:16
Sparse Core Ops, SparseCore 0:
  19.3 57.7 all-gather.1
where the time goes:
time: 236 us; the launch traced here: 234 us
  local copies, waits for them, and re-layouts  78.6 us (33%)
  matrix products  41.4 us (18%)
  waiting for transfers between devices  40.1 us (17%)
  other arithmetic  29.5 us (12%)
  blocking collectives  17.1 us (7%)
  between operations  15.3 us (6%)
  starting transfers between devices  12.4 us (5%)
    all_gather x1, waiting for transfers between devices, on_device(): segment = lax.all_gather(entry_slice, 'ka', axis=0, tiled=True)  20.9 us
    all_to_all x1, waiting for transfers between devices, on_device(): lax.all_to_all(own_entries, 'col', split_axis=0, concat_axis=3, tiled=True)  14.5 us
    all_to_all x1, blocking collectives, on_device(): lax.all_to_all(flat_shard, 'col', split_axis=1, concat_axis=0, tiled=True)  10.6 us
    dot_general x1, matrix products, on_device(): summed = jnp.dot(phases, segment, preferred_element_type=jnp.float32)  9.27 us
    gather x1, local copies, waits for them, and re-layouts, phase_rows(): lattice_rows = jnp.take(lattice, vector_index, axis=0)  8.64 us
    gather x1, local copies, waits for them, and re-layouts, phase_rows(): degree_rows = jnp.take(degrees, vector_index, axis=0)  8.58 us
    all_to_all x1, starting transfers between devices, sent_to_all(): return lax.all_to_all(copies, axis, split_axis=0, concat_axis=0, tiled=True)  7.66 us
    reshape x1, local copies, waits for them, and re-layouts, on_device(): interpolated = regrouped.reshape(quarter, 4, 2, WF, WF)  7.42 us
  transfers between devices with their start and end apart: 3, of which 3 were waited for; matrix products, arithmetic and copies ran while one was open for 22% of the time, Pallas kernels for 0%

commit v1 on v0

--- a/solution.py
+++ b/solution.py
@@ -102,6 +102,33 @@
 
 
 def on_device(hamiltonian, eigvecs, spin, k_indices, r_vectors, degeneracy, fermi_level):
+
+    def lay_the_samples_all(tile_in, on_dim, array_axis):
+        small = lax.axis_size("col")
+        all_values = lax.axis_index("col")
+        extra, response = (small, all_values)
+        answer = tile_in.shape[on_dim] // extra
+        v_now = list(tile_in.shape)
+        v_now[on_dim] = answer
+        h_now = v_now[array_axis]
+        v_now[array_axis] = h_now * extra
+        r2 = jnp.zeros(v_now, tile_in.dtype)
+        ii = 0
+        while ii < extra:
+            fresh = lax.dynamic_slice_in_dim(tile_in, (response ^ ii) * answer, answer, axis=on_dim)
+            if ii:
+                made = []
+                w = 0
+                while w < extra:
+                    made.append((w, w ^ ii))
+                    w = w + 1
+                fresh = lax.ppermute(fresh, "col", made)
+            r2 = lax.dynamic_update_slice_in_dim(
+                r2, fresh, (response ^ ii) * h_now, axis=array_axis
+            )
+            ii += 1
+        return r2
+
     kcount = eigvecs.shape[0]
     col_count = lax.axis_size("col")
     quarter = kcount // col_count
@@ -109,7 +136,7 @@
     vectors = lax.dynamic_slice_in_dim(eigvecs, column * quarter, quarter, 0)
     flat_shard = hamiltonian.reshape(hamiltonian.shape[0] * 2, WF * WF)
     entry_width = WF * WF // col_count
-    entry_slice = lax.all_to_all(flat_shard, "col", split_axis=1, concat_axis=0, tiled=True)
+    entry_slice = lay_the_samples_all(flat_shard, 1, 0)
     segment = lax.all_gather(entry_slice, "ka", axis=0, tiled=True)
     height = segment.shape[0]
     phases = phase_rows(k_indices, r_vectors, degeneracy, height)

time: 236 us -> 239 us (1.013)
  blocking collectives: 17.1 us -> 6.54 us
  waiting for transfers between devices: 40.1 us -> 45 us
  starting transfers between devices: 12.4 us -> 16.8 us
  local copies, waits for them, and re-layouts: 78.6 us -> 82.6 us
    all_to_all x1 -> x0, blocking collectives: 10.6 us -> none  [on_device(): lax.all_to_all(flat_shard, 'col', split_axis=1, concat_axis=0, tiled=True)]
    ppermute x0 -> x3, starting transfers between devices: none -> 4.48 us  [lay_the_samples_all(): fresh = lax.ppermute(fresh, 'col', made)]
    ppermute x0 -> x3, waiting for transfers between devices: none -> 3.43 us  [lay_the_samples_all(): fresh = lax.ppermute(fresh, 'col', made)]
    dynamic_update_slice x0 -> x3, local copies, waits for them, and re-layouts: none -> 2.67 us  [lay_the_samples_all(): lax.dynamic_update_slice_in_dim(r2, fresh, (response ^ ii) * h_now, axis=...]
    unnamed x52 -> x58, local copies, waits for them, and re-layouts: 4.88 us -> 4.89 us
  transfers between devices with their start and end apart: 3 -> 6, of which waited for: 3 -> 5; matrix products, arithmetic and copies ran while one was open for 22% -> 22% of each run, Pallas kernels for 0% -> 0%
where the time goes in v1:
time: 239 us; the launch traced here: 237 us
  local copies, waits for them, and re-layouts  82.6 us (35%)
  waiting for transfers between devices  45 us (19%)
  matrix products  41.5 us (17%)
  other arithmetic  29.5 us (12%)
  starting transfers between devices  16.8 us (7%)
  between operations  15.3 us (6%)
  blocking collectives  6.54 us (3%)
    all_gather x1, waiting for transfers between devices, on_device(): segment = lax.all_gather(entry_slice, 'ka', axis=0, tiled=True)  22.5 us
    all_to_all x1, waiting for transfers between devices, on_device(): lax.all_to_all(own_entries, 'col', split_axis=0, concat_axis=3, tiled=True)  14.5 us
    dot_general x1, matrix products, on_device(): summed = jnp.dot(phases, segment, preferred_element_type=jnp.float32)  9.27 us
    gather x1, local copies, waits for them, and re-layouts, phase_rows(): lattice_rows = jnp.take(lattice, vector_index, axis=0)  8.61 us
    gather x1, local copies, waits for them, and re-layouts, phase_rows(): degree_rows = jnp.take(degrees, vector_index, axis=0)  8.58 us
    all_to_all x1, starting transfers between devices, sent_to_all(): return lax.all_to_all(copies, axis, split_axis=0, concat_axis=0, tiled=True)  7.65 us
    reshape x1, local copies, waits for them, and re-layouts, on_device(): interpolated = regrouped.reshape(quarter, 4, 2, WF, WF)  7.4 us
    all_to_all x1, blocking collectives, sent_to_all(): return lax.all_to_all(copies, axis, split_axis=0, concat_axis=0, tiled=True)  6.54 us
  transfers between devices with their start and end apart: 6, of which 5 were waited for; matrix products, arithmetic and copies ran while one was open for 22% of the time, Pallas kernels for 0%

profile of v1, /device:TPU:1, one launch (start us, length us, event | category | flops | bytes accessed | tf_op | source)
XLA Modules:
  0.0 237.3 jit_solution(4206747079253307424)
XLA Ops:
  7.3 1.9 reshape.801
  9.2 1.7 constant_dynamic-slice_fusion
  10.9 2.0 collective-permute-start
  13.0 2.5 %collective-permute-start.1 = (bf16[16,2304]{1,0:T(8,128)(2,1)}, bf16[16,2304]{1,0:T(8,128)(2,1)}, u32[]{:S(2)}, u32[]{:S(2)}) collective-permute-start(bf16[16,2304]{1,0:T(8,128)(2,1)} %get-tuple-element.20), channel_id=1, source_target_pairs={{0,2},{1,3},{2,0},{3,1},{4,6},{5,7},{6,4},{7,5},{8,10},{9,11},{10,... | collective-permute-start | bytes 221192 | tf_op jit(solution)/shard_map/ppermute | solution.py:125
  15.4 0.9 constant_dynamic-update-slice_fusion.2
  16.3 2.4 %collective-permute-done.1 = bf16[16,2304]{1,0:T(8,128)(2,1)} collective-permute-done((bf16[16,2304]{1,0:T(8,128)(2,1)}, bf16[16,2304]{1,0:T(8,128)(2,1)}, u32[]{:S(2)}, u32[]{:S(2)}) %collective-permute-start.1) | collective-permute-done | bytes 73760 | tf_op jit(solution)/shard_map/ppermute | solution.py:125
  18.7 0.9 constant_dynamic-update-slice_fusion.1
  19.6 1.0 collective-permute-done.2
  20.6 0.9 constant_dynamic-update-slice_fusion
  21.5 0.7 copy-done.19
  22.3 0.8 convert_element_type.177
  23.1 1.0 copy.179
  24.2 8.6 %gather_fusion.1 = s32[2048]{0:T(1024)S(1)} fusion(s32[1024]{0:T(1024)S(1)} %copy-done.2, s32[2048]{0:T(1024)S(1)} %broadcast_clamp_fusion), kind=kCustom, calls=%fused_computation.1 | custom fusion | bytes 24576 | tf_op jit(solution)/shard_map/jit(_take)/gather | solution.py:29
  32.8 8.6 %gather_fusion = s32[2048,3]{1,0:T(8,128)} fusion(s32[1024,3]{1,0:T(8,128)} %copy.179, s32[2048]{0:T(1024)S(1)} %broadcast_clamp_fusion), kind=kCustom, calls=%fused_computation | custom fusion | bytes 57344 | tf_op jit(solution)/shard_map/jit(_take)/gather | solution.py:28
  41.4 2.7 %convert_multiply_fusion = (f32[2048,3]{1,0:T(8,128)}, s32[2048,3]{1,0:T(8,128)}) fusion(f32[2048]{0:T(1024)S(1)} %convert_divide_fusion, s32[2048,3]{1,0:T(8,128)} %gather_fusion, pred[2048]{0:T(1024)(128)(4,1)S(1)} %fusion.93), kind=kLoop, calls=%fused_computation.55 | loop fusion | flops 18432 | bytes 83968 | tf_op jit(solution)/shard_map/mul | solution.py:35
  44.1 1.6 copy.180
  46.0 3.4 %slice_reduce_fusion.2 = (f32[2048]{0:T(1024)S(1)}, f32[2048]{0:T(1024)S(1)}, f32[2048]{0:T(1024)S(1)}) fusion(f32[2048,3]{1,0:T(8,128)} %get-tuple-element.5), kind=kLoop, calls=%fused_computation.54 | loop fusion | bytes 49152 | tf_op jit(solution)/shard_map/slice | solution.py:39
  50.4 1.2 fusion.42
  51.6 2.2 multiply_bitcast_fusion.7
  53.8 2.2 multiply_bitcast_fusion.3
  56.0 1.6 select_convert_fusion.1
  57.6 22.5 %all-gather.2.cloned.1.call-done = bf16[2048,2304]{1,0:T(8,128)(2,1)} async-done(((bf16[64,2304]{1,0:T(8,128)(2,1)}), bf16[2048,2304]{1,0:T(8,128)(2,1)}) %all-gather.2.cloned.1.call-update) | async-done | bytes 9437200 | tf_op jit(solution)/shard_map/all_gather | solution.py:140
  80.1 9.3 %fusion.2 = bf16[64,4,2,2304]{3,0,2,1:T(8,128)(2,1)S(1)} fusion(bf16[2048,2304]{1,0:T(8,128)(2,1)} %all-gather.2.cloned.1.call-done, bf16[64,4,1,2048]{3,0,2,1:T(8,128)(2,1)} %get-tuple-element.8, bf16[64,4,1,2048]{3,0,2,1:T(8,128)(2,1)} %get-tuple-element.7), kind=kOutput, calls=%fused_computation.5 | convolution fusion | flops 4834066432 | bytes 13893632 | tf_op jit(solution)/shard_map/dot_general | solution.py:144
  89.3 3.8 %copy.181 = bf16[64,4,2,2304]{3,2,1,0:T(2,128)(2,1)} copy(bf16[64,4,2,2304]{3,0,2,1:T(8,128)(2,1)S(1)} %fusion.2) | data formatting | bytes 4718592 | tf_op jit(solution)/shard_map/convert_element_type | solution.py:146
  93.2 4.7 %all-to-all-start = ((bf16[64,4,2,2304]{3,2,1,0:T(2,128)(2,1)}), bf16[64,4,2,2304]{3,2,1,0:T(2,128)(2,1)}, u32[]{:S(2)}, u32[]{:S(2)}) async-start(bf16[64,4,2,2304]{3,2,1,0:T(2,128)(2,1)} %copy.181), calls=%async_computation | async-start | bytes 4718592 | tf_op jit(solution)/shard_map/all_to_all | solution.py:147
  97.9 1.1 fusion.37
  99.0 1.0 fusion.24
  100.0 0.8 copy-done.14
  100.7 1.2 fusion.22
  101.9 2.3 copy.197
  104.2 1.3 fusion.45
  105.5 1.2 convolution_subtract_fusion.2
  106.8 2.3 copy.201
  109.9 2.2 fusion.34
  112.2 14.5 %all-to-all-done = bf16[64,4,2,2304]{3,2,1,0:T(2,128)(2,1)} async-done(((bf16[64,4,2,2304]{3,2,1,0:T(2,128)(2,1)}), bf16[64,4,2,2304]{3,2,1,0:T(2,128)(2,1)}, u32[]{:S(2)}, u32[]{:S(2)}) %all-to-all-start) | async-done | bytes 2359328 | tf_op jit(solution)/shard_map/all_to_all | solution.py:147
  126.7 5.0 %copy.254 = bf16[4,16,4,2,2304]{4,0,2,1,3:T(4,128)(2,1)} copy(bf16[4,16,4,2,2304]{4,3,2,1,0:T(2,128)(2,1)} %bitcast.14) | data formatting | bytes 4718592 | tf_op jit(solution)/shard_map/all_to_all | solution.py:147
  131.7 7.4 %reshape.802 = bf16[16,4,2,96,96]{4,3,1,0,2:T(8,128)(2,1)} reshape(bf16[16,4,2,4,2304]{4,3,1,0,2:T(4,128)(2,1)} %bitcast.231) | data formatting | bytes 4718592 | tf_op jit(solution)/shard_map/reshape | solution.py:148
  139.1 2.1 fusion.21
  144.3 2.3 fusion.49
  146.6 2.3 convolution_subtract_fusion
  148.9 3.6 %copy.186 = f32[16,4,96,96]{2,3,1,0:T(8,128)} copy(f32[16,4,96,96]{3,2,1,0:T(8,128)} %convolution_subtract_fusion) | data formatting | bytes 4718592 | tf_op jit(solution)/shard_map/sub | solution.py:71
  152.5 4.7 %convolution_add_fusion = f32[16,4,96,96]{3,2,1,0:T(8,128)} fusion(f32[16,4,96,96]{3,2,1,0:T(8,128)} %fusion.49, bf16[16,4,96,96]{3,2,1,0:T(8,128)(2,1)} %copy-done.10, bf16[64,2,96,96]{3,2,1,0:T(8,128)(2,1)S(1)} %copy-done, s32[]{:T(128)S(6)} %select_n.262, s32[]{:T(128)S(6)} %add.301), kind=kOutput, calls=%fused_computation.32 | convolution fusion | flops 113836032 | bytes 6291464 | tf_op jit(solution)/shard_map/kjn,kcjm->kcnm/dot_general | solution.py:70
  157.2 3.8 %copy.189 = f32[16,4,96,96]{3,2,1,0:T(8,128)} copy(f32[16,4,96,96]{2,3,1,0:T(8,128)} %bitcast.229) | data formatting | bytes 4718592 | tf_op jit(solution)/shard_map/add | solution.py:68
  161.0 5.3 %fusion.18 = (bf16[16,4,1,96,96]{4,3,1,0,2:T(8,128)(2,1)S(1)}, bf16[16,4,1,96,96]{4,3,1,0,2:T(8,128)(2,1)S(1)}) fusion(f32[16,4,96,96]{3,2,1,0:T(8,128)} %copy.189, f32[16,4,96,96]{3,2,1,0:T(8,128)} %convolution_add_fusion, f32[16,4,96,96]{3,2,1,0:T(8,128)S(1)} %copy-done.3, f32[16,4,96,96]{2,3,1,0:T(8,128)} %copy.186), kind=kLoop, calls=%fused_computation.36 | loop fusion | flops 3538944 | bytes 11796480 | tf_op jit(solution)/shard_map/stack | solution.py:76
  166.3 1.1 fusion.36
  167.9 1.9 fusion.25
  170.4 2.0 copy.203
  172.4 3.3 %fusion.12 = bf16[16,3,96,96]{3,2,1,0:T(8,128)(2,1)} fusion(f32[16,3,96,96]{3,2,1,0:T(8,128)S(1)} %convolution_subtract_fusion.1, f32[16,3,96,96]{2,3,1,0:T(8,128)} %copy.203), kind=kLoop, calls=%fused_computation.21 | loop fusion | flops 1327104 | bytes 4423680 | tf_op jit(solution)/shard_map/mul | solution.py:91
  176.2 2.0 copy.208
  178.2 3.1 %subtract_multiply_fusion = bf16[16,3,96,96]{3,2,1,0:T(8,128)(2,1)} fusion(f32[16,3,96,96]{3,2,1,0:T(8,128)} %copy.208, f32[16,3,96,96]{3,2,1,0:T(8,128)S(1)} %convolution_add_fusion.1), kind=kLoop, calls=%fused_computation.24 | loop fusion | flops 1327104 | bytes 4423680 | tf_op jit(solution)/shard_map/mul | solution.py:92
  181.3 4.0 %copy.190 = f32[16,96,96]{0,2,1:T(8,128)} copy(f32[16,96,96]{2,1,0:T(8,128)} %fusion.36) | data formatting | bytes 1179648 | tf_op jit(solution)/shard_map/convert_element_type | solution.py:80
  185.3 2.9 %gather_fusion.2 = f32[96,16]{1,0:T(8,128)S(1)} fusion(f32[16,96,96]{0,2,1:T(8,128)} %copy.190, s32[96]{0:T(128)S(1)} %or_bitcast_fusion), kind=kCustom, calls=%fused_computation.2 | custom fusion | bytes 13056 | tf_op jit(solution)/shard_map/jit(diagonal)/gather | solution.py:80
  188.5 2.0 bitcast_multiply_fusion.2
  190.5 2.8 %copy.209 = bf16[16,96,96,3]{2,3,1,0:T(4,128)(2,1)S(1)} copy(bf16[16,96,96,3]{1,2,3,0:T(8,128)(2,1)} %get-tuple-element.10) | data formatting | bytes 1769472 | tf_op jit(solution)/shard_map/kanm,kbmn,knm->kabn/dot_general | solution.py:97
  193.3 3.9 %copy.204 = bf16[16,96,96,3]{2,3,1,0:T(4,128)(2,1)} copy(bf16[16,96,96,3]{1,2,3,0:T(8,128)(2,1)} %get-tuple-element.9) | data formatting | bytes 1769472 | tf_op jit(solution)/shard_map/kanm,kbmn,knm->kabn/dot_general | solution.py:96
  197.2 1.8 fusion.8
  199.0 5.7 %fusion.5 = (f32[96,3,3]{1,2,0:T(4,128)S(1)}, f32[16,96,3,3]{3,2,1,0:T(4,128)}) fusion(f32[96,16]{0,1:T(8,128)S(1)} %divide_bitcast_fusion, f32[16,96,3,3]{3,2,1,0:T(4,128)S(1)} %fusion.8, bf16[16,96,96,3]{2,3,1,0:T(4,128)(2,1)S(1)} %copy-done.18, bf16[16,3,96,96]{3,2,1,0:T(8,128)(2,1)S(1)} %copy-done.20), kind=kOutput, calls=%fused_computation.7 | convolution fusion | flops 2708640 | bytes 1889664 | tf_op jit(solution)/shard_map/kanm,kbmn,knm->kabn/dot_general | solution.py:96
  205.0 6.5 %all_to_all.25 = f32[4,1,864]{2,1,0:T(1,128)S(1)} all-to-all(f32[4,1,864]{2,1,0:T(1,128)S(1)} %reshape.837), channel_id=1, replica_groups=mesh['ka'=32,'col'=4] {'col'}, dimensions={0} | all-to-all | bytes 27648 | tf_op jit(solution)/shard_map/all_to_all | solution.py:16
  212.0 0.7 reduce.8
  212.8 0.8 reshape.839
  213.7 7.6 %all-to-all-start.2 = ((f32[32,1,864]{2,1,0:T(1,128)}), f32[32,1,864]{2,1,0:T(1,128)S(1)}, u32[]{:S(2)}, u32[]{:S(2)}) async-start(f32[32,1,864]{2,1,0:T(1,128)} %reshape.839), calls=%async_computation.2 | async-start | bytes 229376 | tf_op jit(solution)/shard_map/all_to_all | solution.py:16
  221.3 2.9 %copy.211 = f32[3,3,96,16]{2,3,1,0:T(8,128)} copy(f32[3,3,96,16]{0,1,2,3:T(4,128)} %bitcast.233) | data formatting | bytes 110592 | tf_op jit(solution)/shard_map/mul | solution.py:95
  224.2 4.6 %all-to-all-done.2 = f32[32,1,864]{2,1,0:T(1,128)S(1)} async-done(((f32[32,1,864]{2,1,0:T(1,128)}), f32[32,1,864]{2,1,0:T(1,128)S(1)}, u32[]{:S(2)}, u32[]{:S(2)}) %all-to-all-start.2) | async-done | bytes 110624 | tf_op jit(solution)/shard_map/all_to_all | solution.py:16
  228.8 0.9 reduce.9
  (91 shorter events, 8.2 us)
Async XLA Ops:
  7.2 42.3 %copy-start = (bf16[64,2,96,96]{3,2,1,0:T(8,128)(2,1)S(1)}, bf16[64,2,96,96]{3,2,1,0:T(8,128)(2,1)}, u32[]{:S(2)}) copy-start(bf16[64,2,96,96]{3,2,1,0:T(8,128)(2,1)} %param.8) | copy-start | bytes 7077892
  7.2 15.9 %copy-start.23 = (bf16[2,96,96]{2,1,0:T(8,128)(2,1)S(1)}, bf16[2,96,96]{2,1,0:T(8,128)(2,1)}, u32[]{:S(2)}) copy-start(bf16[2,96,96]{2,1,0:T(8,128)(2,1)} %param.9) | copy-start | bytes 110596
  7.2 15.9 %copy-start.24 = (s32[1024,3]{0,1:T(4,128)S(1)}, s32[1024,3]{0,1:T(4,128)}, u32[]{:S(2)}) copy-start(s32[1024,3]{0,1:T(4,128)} %param.11) | copy-start | bytes 36868
  7.2 16.9 %copy-start.2 = (s32[1024]{0:T(1024)S(1)}, s32[1024]{0:T(1024)}, u32[]{:S(2)}) copy-start(s32[1024]{0:T(1024)} %param.12) | copy-start | bytes 12292
  7.2 72.9 %all-gather.2.cloned.1.call-start = ((), (), s32[]{:S(2)}) async-start(), calls=%async_computation.3 | async-start | bytes 9732096 | tf_op jit(solution)/shard_map/all_gather | solution.py:140
  10.9 4.5 %collective-permute-start = (bf16[16,2304]{1,0:T(8,128)(2,1)}, bf16[16,2304]{1,0:T(8,128)(2,1)}, u32[]{:S(2)}, u32[]{:S(2)}) collective-permute-start(bf16[16,2304]{1,0:T(8,128)(2,1)} %get-tuple-element.21), channel_id=1, source_target_pairs={{0,1},{1,0},{2,3},{3,2},{4,5},{5,4},{6,7},{7,6},{8,9},{9,8},{10,11... | collective-permute-start | bytes 221192 | tf_op jit(solution)/shard_map/ppermute | solution.py:125
  13.0 5.7 %collective-permute-start.1 = (bf16[16,2304]{1,0:T(8,128)(2,1)}, bf16[16,2304]{1,0:T(8,128)(2,1)}, u32[]{:S(2)}, u32[]{:S(2)}) collective-permute-start(bf16[16,2304]{1,0:T(8,128)(2,1)} %get-tuple-element.20), channel_id=1, source_target_pairs={{0,2},{1,3},{2,0},{3,1},{4,6},{5,7},{6,4},{7,5},{8,10},{9,11},{10,... | collective-permute-start | bytes 221192 | tf_op jit(solution)/shard_map/ppermute | solution.py:125
  15.4 5.2 %collective-permute-start.2 = (bf16[16,2304]{1,0:T(8,128)(2,1)}, bf16[16,2304]{1,0:T(8,128)(2,1)}, u32[]{:S(2)}, u32[]{:S(2)}) collective-permute-start(bf16[16,2304]{1,0:T(8,128)(2,1)} %get-tuple-element.19), channel_id=1, source_target_pairs={{0,3},{1,2},{2,1},{3,0},{4,7},{5,6},{6,5},{7,4},{8,11},{9,10},{10,... | collective-permute-start | bytes 221192 | tf_op jit(solution)/shard_map/ppermute | solution.py:125
  21.5 0.7 copy-start.19
  41.4 4.5 %copy-start.25 = (s32[64,3]{0,1:T(4,128)S(1)}, s32[64,3]{0,1:T(4,128)}, u32[]{:S(2)}) copy-start(s32[64,3]{0,1:T(4,128)} %param.10) | copy-start | bytes 2308
  49.5 0.6 copy-start.22
  49.5 4.3 %copy-start.21 = (bf16[96,96]{1,0:T(8,128)(2,1)}, bf16[96,96]{1,0:T(8,128)(2,1)S(1)}, u32[]{:S(2)}) copy-start(bf16[96,96]{1,0:T(8,128)(2,1)S(1)} %get-tuple-element.23) | copy-start | bytes 55300
  93.2 33.5 %all-to-all-start = ((bf16[64,4,2,2304]{3,2,1,0:T(2,128)(2,1)}), bf16[64,4,2,2304]{3,2,1,0:T(2,128)(2,1)}, u32[]{:S(2)}, u32[]{:S(2)}) async-start(bf16[64,4,2,2304]{3,2,1,0:T(2,128)(2,1)} %copy.181), calls=%async_computation | async-start | bytes 4718592 | tf_op jit(solution)/shard_map/all_to_all | solution.py:147
  97.9 2.9 %copy-start.16 = (f32[16,96,96]{2,1,0:T(8,128)S(1)}, f32[16,96,96]{2,1,0:T(8,128)}, u32[]{:S(2)}) copy-start(f32[16,96,96]{2,1,0:T(8,128)} %fusion.42) | copy-start | bytes 1769476
  100.0 0.8 copy-start.14
  109.1 3.0 %copy-start.12 = (f32[16,96,96]{2,1,0:T(8,128)S(1)}, f32[16,96,96]{2,1,0:T(8,128)}, u32[]{:S(2)}) copy-start(f32[16,96,96]{2,1,0:T(8,128)} %convolution_subtract_fusion.2) | copy-start | bytes 1769476
  109.1 3.0 %copy-start.17 = (f32[16,1,96,96]{3,2,0,1:T(8,128)S(1)}, f32[16,1,96,96]{3,2,0,1:T(8,128)}, u32[]{:S(2)}) copy-start(f32[16,1,96,96]{3,2,0,1:T(8,128)} %copy.201) | copy-start | bytes 1769476
  139.1 2.4 copy-start.4
  142.6 1.2 copy-start.10
  157.2 3.8 %copy-start.3 = (f32[16,4,96,96]{3,2,1,0:T(8,128)S(1)}, f32[16,4,96,96]{3,2,1,0:T(8,128)}, u32[]{:S(2)}) copy-start(f32[16,4,96,96]{3,2,1,0:T(8,128)} %convolution_subtract_fusion) | copy-start | bytes 7077892
  161.0 6.4 %copy-start.15 = (bf16[16,96,96,1]{2,1,3,0:T(8,128)(2,1)S(1)}, bf16[16,96,96,1]{2,1,3,0:T(8,128)(2,1)}, u32[]{:S(2)}) copy-start(bf16[16,96,96,1]{2,1,3,0:T(8,128)(2,1)} %fusion.34) | copy-start | bytes 884740
  166.3 1.6 copy-start.5
  166.3 3.5 %copy-start.8 = (bf16[16,4,1,96,96]{4,3,1,0,2:T(8,128)(2,1)}, bf16[16,4,1,96,96]{4,3,1,0,2:T(8,128)(2,1)S(1)}, u32[]{:S(2)}) copy-start(bf16[16,4,1,96,96]{4,3,1,0,2:T(8,128)(2,1)S(1)} %get-tuple-element.28) | copy-start | bytes 3538948
  172.4 3.4 %copy-start.6 = (bf16[16,4,1,96,96]{4,3,1,0,2:T(8,128)(2,1)S(1)}, bf16[16,4,1,96,96]{4,3,1,0,2:T(8,128)(2,1)}, u32[]{:S(2)}) copy-start(bf16[16,4,1,96,96]{4,3,1,0,2:T(8,128)(2,1)} %copy-done.5) | copy-start | bytes 3538948
  172.4 3.4 %copy-start.11 = (f32[16,3,96,96]{3,2,1,0:T(8,128)S(1)}, f32[16,3,96,96]{3,2,1,0:T(8,128)}, u32[]{:S(2)}) copy-start(f32[16,3,96,96]{3,2,1,0:T(8,128)} %fusion.25) | copy-start | bytes 5308420
  181.3 7.2 %copy-start.7 = (bf16[16,4,1,96,96]{4,3,1,0,2:T(8,128)(2,1)S(1)}, bf16[16,4,1,96,96]{4,3,1,0,2:T(8,128)(2,1)}, u32[]{:S(2)}) copy-start(bf16[16,4,1,96,96]{4,3,1,0,2:T(8,128)(2,1)} %copy-done.5) | copy-start | bytes 3538948
  181.3 7.2 %copy-start.9 = (bf16[16,4,1,96,96]{4,3,1,0,2:T(8,128)(2,1)S(1)}, bf16[16,4,1,96,96]{4,3,1,0,2:T(8,128)(2,1)}, u32[]{:S(2)}) copy-start(bf16[16,4,1,96,96]{4,3,1,0,2:T(8,128)(2,1)} %copy-done.8) | copy-start | bytes 3538948
  190.5 6.7 %copy-start.13 = (bf16[16,3,96,96]{3,2,1,0:T(8,128)(2,1)S(1)}, bf16[16,3,96,96]{3,2,1,0:T(8,128)(2,1)}, u32[]{:S(2)}) copy-start(bf16[16,3,96,96]{3,2,1,0:T(8,128)(2,1)} %subtract_multiply_fusion) | copy-start | bytes 2654212
  197.2 1.8 copy-start.18
  197.2 1.8 copy-start.20
  212.8 17.7 %copy-start.1 = (bf16[64,2,96,96]{3,2,1,0:T(8,128)(2,1)S(1)}, bf16[64,2,96,96]{3,2,1,0:T(8,128)(2,1)}, u32[]{:S(2)}) copy-start(bf16[64,2,96,96]{3,2,1,0:T(8,128)(2,1)} %param.8) | copy-start | bytes 7077892
  213.7 15.1 %all-to-all-start.2 = ((f32[32,1,864]{2,1,0:T(1,128)}), f32[32,1,864]{2,1,0:T(1,128)S(1)}, u32[]{:S(2)}, u32[]{:S(2)}) async-start(f32[32,1,864]{2,1,0:T(1,128)} %reshape.839), calls=%async_computation.2 | async-start | bytes 229376 | tf_op jit(solution)/shard_map/all_to_all | solution.py:16
Sparse Core Ops, SparseCore 0:
  22.4 57.6 all-gather.1
